TPU v7x, 256 devices: a whole 4x4x8 slice. The times are simulated.
256 devices in a mesh: row: 32 (over y, z), col: 8 (over x, core).
Axes of the slice: x: 4, y: 4, z: 8, core: 2. Of those that a mesh axis runs over, the one named last changes fastest.
Arguments:
- layer_input: bfloat16 [8192, 8192], P('row'), may hold values from -7 to 7
- gain: float32 [8192], replicated, may hold values from 0.5 to 6
- d_query: bfloat16 [8192, 4096], P('row', 'col'), may hold values from -6 to 6
- d_keyval: bfloat16 [8192, 2048], P('row', 'col'), may hold values from -6 to 6
- w_query: bfloat16 [8192, 4096], P('row', 'col'), may hold values from -0.0625 to 0.0625
- w_keyval: bfloat16 [8192, 2048], P('row', 'col'), may hold values from -1 to 1
- d_resid: bfloat16 [8192, 8192], P('row', 'col'), may hold values from -6 to 6
Outputs:
- d_input: bfloat16 [8192, 8192], P('row', 'col')
- grad_wq: bfloat16 [8192, 4096], P('row', 'col')
- grad_wkv: bfloat16 [8192, 2048], P('row', 'col')
- grad_gain: float32 [8192], P('col')
- grad_square_sum: float32 [], replicated
All inputs are finite; a program needn't handle non-finite values.
Results may differ from a plain program's by a relative error of at most 0.023.
Values may be sent and summed in bfloat16 or wider, within the bound.
No kernel may reach another device: no remote copies, remote signals or barrier semaphores. Data moves between devices by JAX's collectives and lax.ppermute only.
A program may use at most 128 MiB of HBM per device.

v0:
```python
import math

import jax
import jax.numpy as jnp
from jax import lax
from jax.sharding import Mesh
from jax.sharding import PartitionSpec as P

ROW = ("row_0", "row_1")


epsilon = 1e-05


def in_one_piece(arrays, axis, dim, along):
    both = jnp.concatenate(arrays, axis=along)
    whole, at, gathered = (lax.all_gather(both, axis, axis=dim, tiled=True), 0, [])
    for a in arrays:
        gathered.append(lax.slice_in_dim(whole, at, at + a.shape[along], axis=along))
        at += a.shape[along]
    return tuple(gathered)


def cut_along(shard, dim, count):
    dims = shard.shape
    pieces = shard.reshape(*dims[:dim], count, dims[dim] // count, *dims[dim + 1 :])
    return jnp.moveaxis(pieces, dim, 0)


def summed_on_arrival(shard, axis, dim):
    count = lax.axis_size(axis)
    pieces = lax.all_to_all(cut_along(shard, dim, count), axis, 0, 0, tiled=True)
    return jnp.sum(pieces.astype(jnp.float32), axis=0)


def summed_rows(terms, axes):
    subtotal = terms.astype(jnp.bfloat16)
    for axis in axes:
        subtotal = lax.psum_scatter(subtotal, axis, scatter_dimension=0, tiled=True)
    return subtotal.astype(jnp.float32)


def copy_for_each(shard, axis):
    copies = jnp.broadcast_to(shard, (lax.axis_size(axis), *shard.shape))
    return lax.all_to_all(copies, axis, split_axis=0, concat_axis=0, tiled=True)


def of_everyone(shard, axis):
    return copy_for_each(shard, axis).sum(axis=0)


def packed_total(arrays, axis):
    vector, at, gathered = (jnp.concatenate([a.reshape(-1) for a in arrays]), 0, [])
    subtotal = of_everyone(vector, axis)
    for a in arrays:
        gathered.append(subtotal[at : at + a.size].reshape(a.shape))
        at += a.size
    return tuple(gathered)


def local(layer_input, gain, d_query, d_keyval, w_query, w_keyval, d_resid):
    inputs = layer_input.astype(jnp.float32)
    inv_rms = lax.rsqrt(jnp.mean(inputs * inputs, axis=1, keepdims=True) + epsilon)
    normed = (inputs * inv_rms * gain).astype(jnp.bfloat16)
    model_width = inputs.shape[1]
    local_tokens = inputs.shape[0]
    tokens_all = local_tokens * lax.axis_size(ROW)
    scaling = 1.0 / math.sqrt(tokens_all)
    weight_scale = 1.0 / math.sqrt(local_tokens)
    contract_cols = (((1,), (1,)), ((), ()))
    pieces = in_one_piece((w_query, w_keyval), ROW, 0, 1)
    partial_value = lax.dot_general(
        d_query, pieces[0], contract_cols, preferred_element_type=jnp.float32
    )
    partial_value = partial_value + lax.dot_general(
        d_keyval, pieces[1], contract_cols, preferred_element_type=jnp.float32
    )
    rounded = lax.optimization_barrier(partial_value.astype(jnp.bfloat16)).astype(jnp.float32)
    feature_grad = summed_on_arrival(rounded.astype(jnp.bfloat16), "col", 1)
    slice_width = feature_grad.shape[1]
    col_start = lax.axis_index("col") * slice_width
    input_part = lax.dynamic_slice_in_dim(inputs, col_start, slice_width, 1)
    gain_part = lax.dynamic_slice_in_dim(gain, col_start, slice_width, 0)
    weighted = gain_part * feature_grad
    token_dot = lax.psum(jnp.sum(weighted * input_part, axis=1, keepdims=True), "col")
    d_input = (
        d_resid.astype(jnp.float32)
        + inv_rms * weighted
        - input_part * inv_rms**3 * token_dot / model_width
    ).astype(jnp.bfloat16)
    gain_partial = jnp.sum(feature_grad * input_part * inv_rms, axis=0) * scaling
    cotangent = jnp.concatenate([d_query, d_keyval], axis=1)
    query_cols = d_query.shape[1]
    contract_rows = (((0,), (0,)), ((), ()))
    summed = summed_rows(
        lax.dot_general(normed, cotangent, contract_rows, preferred_element_type=jnp.float32)
        * weight_scale,
        ROW,
    )
    grad_wq = summed[:, :query_cols].astype(jnp.bfloat16)
    grad_wkv = summed[:, query_cols:].astype(jnp.bfloat16)
    query_f = grad_wq.astype(jnp.float32)
    keyval_f = grad_wkv.astype(jnp.float32)
    tile_square = jnp.sum(query_f * query_f) + jnp.sum(keyval_f * keyval_f)
    grad_gain, row_square = packed_total((gain_partial, tile_square), ROW)
    grand_total = lax.psum(row_square + jnp.sum(grad_gain * grad_gain), "col")
    grad_square_sum = grand_total / jnp.float32(model_width)
    return (d_input, grad_wq, grad_wkv, grad_gain, grad_square_sum)


def solution(mesh):
    torus = Mesh(mesh.devices.reshape(4, 8, mesh.shape["col"]), ("row_0", "row_1", "col"))
    in_specs = (
        P(ROW, None),
        P(),
        P(ROW, "col"),
        P(ROW, "col"),
        P(ROW, "col"),
        P(ROW, "col"),
        P(ROW, "col"),
    )
    out_specs = (P(ROW, "col"), P(ROW, "col"), P(ROW, "col"), P("col"), P())
    return jax.shard_map(local, mesh=torus, in_specs=in_specs, out_specs=out_specs, check_vma=False)
```

profile of v0, /device:TPU:1, one launch (start us, length us, event | category | flops | bytes accessed | tf_op | source)
XLA Modules:
  0.0 347.9 jit_solution(13555276009178448421)
XLA Ops:
  8.0 0.0 reduce-scatter.3.cloned.1.call-start
  8.1 6.4 %copy.19 = bf16[256,8192]{0,1:T(8,128)(2,1)} copy(bf16[256,8192]{1,0:T(8,128)(2,1)} %param.7) | data formatting | bytes 8388608 | tf_op args[0]
  14.5 3.3 multiply_reduce_fusion
  17.8 8.1 %multiply_convert_fusion = bf16[8192,768]{1,0:T(8,128)(2,1)} fusion(f32[8192]{0:T(1024)S(1)} %copy-done.6, f32[256]{0:T(256)S(1)} %get-tuple-element.31, bf16[256,8192]{0,1:T(8,128)(2,1)} %copy.19, bf16[256,256]{1,0:T(8,128)(2,1)S(1)} %copy-done.4, bf16[256,512]{1,0:T(8,128)(2,1)S(1)} %copy-done.2), kind=kOutput, calls=%fused_computation | convolution fusion | flops 3242983424 | bytes 17204224 | tf_op jit(solution)/shard_map/dot_general | solution.py:96
  26.0 0.0 all-gather.2.cloned.1.call-start
  26.0 0.9 copy-done.3
  26.9 0.0 copy-done.5
  26.9 0.8 pad_maximum_fusion
  27.7 0.0 reduce-scatter.5.cloned.1.call-start
  27.8 142.4 %reduce-scatter.3.cloned.1.call-done = bf16[2048,768]{1,0:T(8,128)(2,1)} async-done(((bf16[8192,768]{1,0:T(8,128)(2,1)}), bf16[2048,768]{1,0:T(8,128)(2,1)}) %reduce-scatter.3.cloned.1.call-update) | async-done | bytes 3145744 | tf_op jit(solution)/shard_map/reduce_scatter | solution.py:39
  170.1 56.0 %all-gather.2.cloned.1.call-done = bf16[8192,768]{1,0:T(8,128)(2,1)} async-done(((bf16[256,768]{1,0:T(8,128)(2,1)}), bf16[8192,768]{1,0:T(8,128)(2,1)}) %all-gather.2.cloned.1.call-update) | async-done | bytes 12582928 | tf_op jit(solution)/shard_map/all_gather | solution.py:17
  226.2 6.0 %fusion.2 = f32[8192,256]{1,0:T(8,128)S(1)} fusion(bf16[256,512]{1,0:T(8,128)(2,1)S(1)} %copy-done.2, bf16[8192,768]{1,0:T(8,128)(2,1)} %all-gather.2.cloned.1.call-done), kind=kOutput, calls=%fused_computation.4 | convolution fusion | flops 2147483648 | bytes 17039360 | tf_op jit(solution)/shard_map/dot_general | solution.py:72
  232.2 1.2 copy-done
  233.4 3.2 fusion.1
  236.6 5.6 %all-to-all-start = ((bf16[8,256,1024]{1,2,0:T(8,128)(2,1)}), bf16[8,256,1024]{1,2,0:T(8,128)(2,1)}, u32[]{:S(2)}, u32[]{:S(2)}) async-start(bf16[8,256,1024]{1,2,0:T(8,128)(2,1)} %bitcast.9), calls=%async_computation | async-start | bytes 8388608 | tf_op jit(solution)/shard_map/all_to_all | solution.py:32
  242.2 6.1 %convert_element_type.36 = f32[256,8192]{0,1:T(8,128)} convert(bf16[256,8192]{0,1:T(8,128)(2,1)} %copy.19) | non-fusion elementwise | flops 2097152 | bytes 12582912 | tf_op jit(solution)/shard_map/convert_element_type | solution.py:62
  248.4 42.7 %all-to-all-done = bf16[8,256,1024]{1,2,0:T(8,128)(2,1)} async-done(((bf16[8,256,1024]{1,2,0:T(8,128)(2,1)}), bf16[8,256,1024]{1,2,0:T(8,128)(2,1)}, u32[]{:S(2)}, u32[]{:S(2)}) %all-to-all-start) | async-done | bytes 4194336 | tf_op jit(solution)/shard_map/all_to_all | solution.py:32
  291.1 2.9 convert_reduce_fusion
  293.9 1.7 multiply_reduce_fusion.1
  295.6 0.0 reduce-scatter.5.cloned.1.call-done
  295.6 2.3 multiply_reduce_fusion.3
  297.9 2.2 multiply_reduce_fusion.4
  301.4 0.7 broadcast_in_dim.10
  302.1 6.9 %all-to-all-start.1 = ((f32[32,1,1025]{2,1,0:T(1,128)}), f32[32,1,1025]{2,1,0:T(1,128)S(1)}, u32[]{:S(2)}, u32[]{:S(2)}) async-start(f32[32,1,1025]{2,1,0:T(1,128)} %broadcast_in_dim.10), calls=%async_computation.3 | async-start | bytes 294912 | tf_op jit(solution)/shard_map/all_to_all | solution.py:45
  309.0 0.2 copy.18
  309.2 9.0 %all-to-all-done.1 = f32[32,1,1025]{2,1,0:T(1,128)S(1)} async-done(((f32[32,1,1025]{2,1,0:T(1,128)}), f32[32,1,1025]{2,1,0:T(1,128)S(1)}, u32[]{:S(2)}, u32[]{:S(2)}) %all-to-all-start.1) | async-done | bytes 131232 | tf_op jit(solution)/shard_map/all_to_all | solution.py:45
  318.2 0.1 reduce_sum.78
  318.3 0.5 slice.31
  318.9 1.2 multiply_reduce_fusion.5
  321.3 14.8 %all-reduce = (f32[256]{0:T(256)S(1)}, f32[]{:T(128)}) all-reduce(f32[256]{0:T(256)S(1)} %get-tuple-element.21, f32[]{:T(128)S(6)} %add.45), channel_id=1, replica_groups=mesh['row_0'=4,'row_1'=8,'col'=8] {'col'}, use_global_device_ids=true, to_apply=%region_3.0 | all-reduce | flops 257 | bytes 2056 | tf_op jit(solution)/shard_map/psum | solution.py:85
  336.1 1.5 subtract_convert_fusion
  337.7 1.0 copy.21
  (18 shorter events, 0.1 us)
Async XLA Ops:
  8.0 9.8 %copy-start.2 = (bf16[256,512]{1,0:T(8,128)(2,1)S(1)}, bf16[256,512]{1,0:T(8,128)(2,1)}, u32[]{:S(2)}) copy-start(bf16[256,512]{1,0:T(8,128)(2,1)} %param.9) | copy-start | bytes 786436
  8.0 9.8 %copy-start.4 = (bf16[256,256]{1,0:T(8,128)(2,1)S(1)}, bf16[256,256]{1,0:T(8,128)(2,1)}, u32[]{:S(2)}) copy-start(bf16[256,256]{1,0:T(8,128)(2,1)} %param.10) | copy-start | bytes 393220
  8.0 9.8 %copy-start.6 = (f32[8192]{0:T(1024)S(1)}, f32[8192]{0:T(1024)}, u32[]{:S(2)}) copy-start(f32[8192]{0:T(1024)} %param.8) | copy-start | bytes 98308
  8.0 162.1 %reduce-scatter.3.cloned.1.call-start = ((), (), s32[]{:S(2)}) async-start(), calls=%async_computation.5 | async-start | bytes 15728640 | tf_op jit(solution)/shard_map/reduce_scatter | solution.py:39
  25.9 0.9 copy-start.3
  25.9 1.0 copy-start.5
  26.0 200.2 %all-gather.2.cloned.1.call-start = ((), (), s32[]{:S(2)}) async-start(), calls=%async_computation.4 | async-start | bytes 12976128 | tf_op jit(solution)/shard_map/all_gather | solution.py:17
  27.7 267.9 %reduce-scatter.5.cloned.1.call-start = ((), (), s32[]{:S(2)}) async-start(), calls=%async_computation.6 | async-start | bytes 3538944 | tf_op jit(solution)/shard_map/reduce_scatter | solution.py:39
  226.2 7.2 %copy-start = (bf16[8192,768]{1,0:T(8,128)(2,1)S(1)}, bf16[8192,768]{1,0:T(8,128)(2,1)}, u32[]{:S(2)}) copy-start(bf16[8192,768]{1,0:T(8,128)(2,1)} %all-gather.2.cloned.1.call-done) | copy-start | bytes 37748740
  236.6 54.4 %all-to-all-start = ((bf16[8,256,1024]{1,2,0:T(8,128)(2,1)}), bf16[8,256,1024]{1,2,0:T(8,128)(2,1)}, u32[]{:S(2)}, u32[]{:S(2)}) async-start(bf16[8,256,1024]{1,2,0:T(8,128)(2,1)} %bitcast.9), calls=%async_computation | async-start | bytes 8388608 | tf_op jit(solution)/shard_map/all_to_all | solution.py:32
  242.2 66.8 %copy-start.1 = (bf16[256,1024]{1,0:T(8,128)(2,1)S(1)}, bf16[256,1024]{1,0:T(8,128)(2,1)}, u32[]{:S(2)}) copy-start(bf16[256,1024]{1,0:T(8,128)(2,1)} %param.13) | copy-start | bytes 1572868
  302.1 16.1 %all-to-all-start.1 = ((f32[32,1,1025]{2,1,0:T(1,128)}), f32[32,1,1025]{2,1,0:T(1,128)S(1)}, u32[]{:S(2)}, u32[]{:S(2)}) async-start(f32[32,1,1025]{2,1,0:T(1,128)} %broadcast_in_dim.10), calls=%async_computation.3 | async-start | bytes 294912 | tf_op jit(solution)/shard_map/all_to_all | solution.py:45
Sparse Core Ops, SparseCore 0:
  26.1 143.9 reduce-scatter.2
  172.7 70.0 reduce-scatter.4
Sparse Core Ops, SparseCore 1:
  29.6 196.5 all-gather.1
where the time goes:
time: 349 us; the launch traced here: 348 us
  waiting for transfers between devices  250 us (72%)
  other arithmetic  22.1 us (6%)
  between operations  20 us (6%)
  matrix products  17.3 us (5%)
  blocking collectives  14.8 us (4%)
  starting transfers between devices  12.6 us (4%)
  local copies, waits for them, and re-layouts  11 us (3%)
    reduce_scatter x2, waiting for transfers between devices, summed_rows(): subtotal = lax.psum_scatter(subtotal, axis, scatter_dimension=0, tiled=True)  142 us
    all_gather x1, waiting for transfers between devices, in_one_piece(): lax.all_gather(both, axis, axis=dim, tiled=True)  56 us
    all_to_all x1, waiting for transfers between devices, summed_on_arrival(): lax.all_to_all(cut_along(shard, dim, count), axis, 0, 0, tiled=True)  42.7 us
    psum x1, blocking collectives, local(): lax.psum(jnp.sum(weighted * input_part, axis=1, keepdims=True), 'col')  14.8 us
    unnamed x17, local copies, waits for them, and re-layouts  9.76 us
    all_to_all x1, waiting for transfers between devices, copy_for_each(): return lax.all_to_all(copies, axis, split_axis=0, concat_axis=0, tiled=True)  8.99 us
    dot_general x1, matrix products, local(): lax.dot_general(normed, cotangent, contract_rows, preferred_element_type=...  8.09 us
  transfers between devices with their start and end apart: 5, of which 4 were waited for; matrix products, arithmetic and copies ran while one was open for 6% of the time, Pallas kernels for 0%

commit v1 on v0

v1 whole, which is shorter than its diff:
```python
import math

import jax
import jax.numpy as jnp
from jax import lax
from jax.sharding import Mesh
from jax.sharding import PartitionSpec as P

ROW = ("y", "z")
COL = ("x", "k")
f32 = jnp.float32
bf16 = jnp.bfloat16

epsilon = 1e-05


def copies(block, axis):
    count = lax.axis_size(axis)
    spread = jnp.broadcast_to(block[None], (count, *block.shape))
    return lax.all_to_all(spread, axis, 0, 0, tiled=True)


def local(layer_input, gain, d_query, d_keyval, w_query, w_keyval, d_resid):
    ny, nz, nx, nk = (lax.axis_size(a) for a in ("y", "z", "x", "k"))
    y, z, x, k = (lax.axis_index(a) for a in ("y", "z", "x", "k"))
    tokens, width = layer_input.shape
    all_tokens = tokens * ny * nz
    part = width // ny
    half = part // nk
    rows = part // nz
    query_cols = d_query.shape[1]
    col = x * nk + k

    w_tile = jnp.concatenate([w_query, w_keyval], axis=1)
    w_part = lax.all_gather(w_tile, "z", axis=0, tiled=True)
    d_tile = jnp.concatenate([d_query, d_keyval], axis=1)
    d_part = copies(d_tile, "y")
    columns = d_tile.shape[1]

    share = tokens // (nx * nk)
    mine = lax.dynamic_slice_in_dim(layer_input, col * share, share, 0).astype(f32)
    scale = lax.rsqrt(jnp.mean(mine * mine, axis=1, keepdims=True) + epsilon)
    normed = (mine * scale * gain).astype(bf16)
    normed = jnp.moveaxis(normed.reshape(share, ny, part), 1, 0)
    normed = lax.all_to_all(normed, "y", 0, 0, tiled=True)
    normed = lax.all_gather(normed[None], COL, axis=0, tiled=True)

    d_rows = d_part.reshape(ny * tokens, columns)
    contract_cols = (((1,), (1,)), ((), ()))
    w_other = lax.dynamic_slice_in_dim(w_part, (1 - k) * half, half, 0)
    w_own = lax.dynamic_slice_in_dim(w_part, k * half, half, 0)
    other = lax.dot_general(d_rows, w_other, contract_cols, preferred_element_type=f32)
    other = lax.ppermute(other.astype(bf16), "k", [(0, 1), (1, 0)])
    own = lax.dot_general(d_rows, w_own, contract_cols, preferred_element_type=f32)
    both = (own + other.astype(f32)).astype(bf16).reshape(ny, tokens, half)
    pieces = lax.all_to_all(both, "x", 0, 0, tiled=True)
    summed = jnp.sum(pieces.astype(f32), axis=0).astype(bf16)
    swap = [(a * nx + b, b * nx + a) for a in range(ny) for b in range(nx)]
    feature_grad = lax.ppermute(summed, ("y", "x"), swap).astype(f32)

    inputs = layer_input.astype(f32)
    inv_rms = lax.rsqrt(jnp.mean(inputs * inputs, axis=1, keepdims=True) + epsilon)
    input_part = lax.dynamic_slice_in_dim(layer_input, col * half, half, 1).astype(f32)
    gain_part = lax.dynamic_slice_in_dim(gain, col * half, half, 0)
    weighted = gain_part * feature_grad
    dots = jnp.sum(weighted * input_part, axis=1)
    token_dot = jnp.sum(copies(dots, COL), axis=0)[:, None]
    d_input = (
        d_resid.astype(f32)
        + inv_rms * weighted
        - input_part * inv_rms**3 * token_dot / width
    ).astype(bf16)

    d_sorted = jnp.moveaxis(d_part.reshape(ny, nx * nk, share, columns), 1, 0)
    weight_scale = 1.0 / math.sqrt(tokens)
    tile_partial = lax.dot_general(
        normed.reshape(nx * nk * ny * share, part),
        d_sorted.reshape(nx * nk * ny * share, columns),
        (((0,), (0,)), ((), ())),
        preferred_element_type=f32,
    )
    tile_partial = (tile_partial * weight_scale).astype(bf16)
    tile = lax.psum_scatter(tile_partial, "z", scatter_dimension=0, tiled=True)
    grad_wq = tile[:, :query_cols]
    grad_wkv = tile[:, query_cols:]
    tile_f = tile.astype(f32)
    tile_square = jnp.sum(tile_f * tile_f)

    row = y * nz + z
    gain_row = lax.dynamic_slice_in_dim(gain, row * rows, rows, 0)
    gain_scale = 1.0 / (weight_scale * math.sqrt(all_tokens))
    gain_terms = jnp.sum(tile_f * w_tile.astype(f32), axis=1) * gain_scale / gain_row
    packed = jnp.concatenate([gain_terms, jnp.broadcast_to(tile_square, (128,))])
    packed = jnp.sum(copies(packed.reshape(-1, 128), COL), axis=0)
    packed = copies(packed, ROW)
    packed = packed.reshape(ny * nz, rows + 128)
    gains = packed[:, :rows].reshape(width)
    grand_total = jnp.sum(packed[:, rows]) + jnp.sum(gains * gains)
    grad_square_sum = grand_total / f32(width)
    grad_gain = lax.dynamic_slice_in_dim(gains, col * half, half, 0)
    return (d_input, grad_wq, grad_wkv, grad_gain, grad_square_sum)


def solution(mesh):
    torus = Mesh(mesh.devices.reshape(4, 8, 4, 2), ("y", "z", "x", "k"))
    both = P(ROW, COL)
    in_specs = (P(ROW, None), P(), both, both, both, both, both)
    out_specs = (both, both, both, P(COL), P())
    return jax.shard_map(local, mesh=torus, in_specs=in_specs, out_specs=out_specs, check_vma=False)
```

time: 349 us -> 229 us (0.66)
  waiting for transfers between devices: 250 us -> 70.3 us
  blocking collectives: 14.8 us -> 62.8 us
  starting transfers between devices: 12.6 us -> 42.2 us
  other arithmetic: 22.1 us -> 13.8 us
  local copies, waits for them, and re-layouts: 11 us -> 6.78 us
  between operations: 20 us -> 16.4 us
    reduce_scatter x2 -> x1, waiting for transfers between devices: 142 us -> 0.01 us  [local(): tile = lax.psum_scatter(tile_partial, 'z', scatter_dimension=0, tiled=True)]
    all_to_all x0 -> x3, blocking collectives: none -> 62.8 us  [the longest x1 29.2 us: local(): pieces = lax.all_to_all(both, 'x', 0, 0, tiled=True)]
    all_to_all x2 -> x3, waiting for transfers between devices: 51.6 us -> 11.1 us  [copies(): return lax.all_to_all(spread, axis, 0, 0, tiled=True)]
    all_to_all x2 -> x3, starting transfers between devices: 12.5 us -> 40 us  [copies(): return lax.all_to_all(spread, axis, 0, 0, tiled=True)]
    psum x1 -> x0, blocking collectives: 14.8 us -> none  [local(): lax.psum(jnp.sum(weighted * input_part, axis=1, keepdims=True), 'col')]
    unnamed x17 -> x19, local copies, waits for them, and re-layouts: 9.76 us -> 0.81 us
    convert_element_type x2, other arithmetic: 7.7 us -> 3.52 us  [the longest x1 2.26 us: local(): d_input = (d_resid.astype(f32) + inv_rms * weighted - input_part * inv_rm...]
    ppermute x0 -> x2, waiting for transfers between devices: none -> 4.13 us  [the longest x1 4.13 us: local(): other = lax.ppermute(other.astype(bf16), 'k', [(0, 1), (1, 0)])]
  transfers between devices with their start and end apart: 5 -> 8, of which waited for: 4 -> 6; matrix products, arithmetic and copies ran while one was open for 6% -> 13% of each run, Pallas kernels for 0% -> 0%
where the time goes in v1:
time: 229 us; the launch traced here: 228 us
  waiting for transfers between devices  70.3 us (31%)
  blocking collectives  62.8 us (27%)
  starting transfers between devices  42.2 us (18%)
  between operations  16.4 us (7%)
  matrix products  15.9 us (7%)
  other arithmetic  13.8 us (6%)
  local copies, waits for them, and re-layouts  6.78 us (3%)
    all_to_all x3, starting transfers between devices, copies(): return lax.all_to_all(spread, axis, 0, 0, tiled=True)  40 us
    all_gather x1, waiting for transfers between devices, local(): w_part = lax.all_gather(w_tile, 'z', axis=0, tiled=True)  38.9 us
    all_to_all x1, blocking collectives, local(): pieces = lax.all_to_all(both, 'x', 0, 0, tiled=True)  29.2 us
    all_to_all x1, blocking collectives, copies(): return lax.all_to_all(spread, axis, 0, 0, tiled=True)  20.7 us
    all_gather x1, waiting for transfers between devices, local(): normed = lax.all_gather(normed[None], COL, axis=0, tiled=True)  16.1 us
    all_to_all x1, blocking collectives, local(): normed = lax.all_to_all(normed, 'y', 0, 0, tiled=True)  12.8 us
    all_to_all x3, waiting for transfers between devices, copies(): return lax.all_to_all(spread, axis, 0, 0, tiled=True)  11.1 us
    dot_general x1, matrix products, local(): lax.dot_general(normed.reshape(nx * nk * ny * share, part), d_sorted.resh...  7.44 us
  transfers between devices with their start and end apart: 8, of which 6 were waited for; matrix products, arithmetic and copies ran while one was open for 13% of the time, Pallas kernels for 0%

profile of v1, /device:TPU:1, one launch (start us, length us, event | category | flops | bytes accessed | tf_op | source)
XLA Modules:
  0.0 228.2 jit_solution(10326359306559269971)
XLA Ops:
  7.3 1.3 fusion.13
  8.6 1.3 fusion.15
  10.5 12.8 %all_to_all.31 = bf16[4,32,2048]{2,1,0:T(8,128)(2,1)} all-to-all(bf16[4,32,2048]{2,1,0:T(8,128)(2,1)S(1)} %copy.23), channel_id=1, replica_groups=mesh['y'=4,'z'=8,'x'=4,'k'=2] {'y'}, dimensions={0} | all-to-all | bytes 1048576 | tf_op jit(solution)/shard_map/all_to_all | solution.py:45
  23.5 0.7 copy-done
  24.5 20.7 %all_to_all.32 = bf16[4,256,768]{2,1,0:T(8,128)(2,1)S(1)} all-to-all(bf16[4,256,768]{2,1,0:T(8,128)(2,1)S(1)} %broadcast_in_dim.12), channel_id=1, replica_groups=mesh['y'=4,'z'=8,'x'=4,'k'=2] {'y'}, dimensions={0} | all-to-all | bytes 3145728 | tf_op jit(solution)/shard_map/all_to_all | solution.py:20
  45.2 16.1 %all-gather.6.cloned.1.call-done = bf16[32,32,2048]{2,1,0:T(8,128)(2,1)} async-done(((bf16[4,32,2048]{2,1,0:T(8,128)(2,1)}), bf16[32,32,2048]{2,1,0:T(8,128)(2,1)}) %all-gather.6.cloned.1.call-update) | async-done | bytes 4194320 | tf_op jit(solution)/shard_map/all_gather | solution.py:46
  61.3 7.4 %fusion = bf16[2048,768]{1,0:T(8,128)(2,1)} fusion(bf16[8,4,32,2048]{3,2,1,0:T(8,128)(2,1)} %bitcast.35, bf16[4,8,32,768]{3,2,1,0:T(8,128)(2,1)S(1)} %bitcast.28), kind=kOutput, calls=%fused_computation.2 | convolution fusion | flops 3224371200 | bytes 8912896 | tf_op jit(solution)/shard_map/dot_general | solution.py:76
  68.8 38.9 %all-gather.4.cloned.1.call-done = bf16[2048,768]{1,0:T(8,128)(2,1)} async-done(((bf16[256,768]{1,0:T(8,128)(2,1)}), bf16[2048,768]{1,0:T(8,128)(2,1)}) %all-gather.4.cloned.1.call-update) | async-done | bytes 3145744 | tf_op jit(solution)/shard_map/all_gather | solution.py:35
  107.7 4.5 %convolution_convert_fusion = bf16[1024,1024]{1,0:T(8,128)(2,1)} fusion(bf16[1024,768]{1,0:T(8,128)(2,1)S(1)} %bitcast.29, bf16[2048,768]{1,0:T(8,128)(2,1)} %all-gather.4.cloned.1.call-done, s32[]{:T(128)S(6)} %select_n.19), kind=kOutput, calls=%fused_computation.4 | convolution fusion | flops 1611661312 | bytes 5242884 | tf_op jit(solution)/shard_map/dot_general | solution.py:52
  112.2 1.2 collective-permute-start
  113.5 4.1 %collective-permute-done = bf16[1024,1024]{1,0:T(8,128)(2,1)} collective-permute-done((bf16[1024,1024]{1,0:T(8,128)(2,1)}, bf16[1024,1024]{1,0:T(8,128)(2,1)}, u32[]{:S(2)}, u32[]{:S(2)}) %collective-permute-start) | collective-permute-done | bytes 2097184 | tf_op jit(solution)/shard_map/ppermute | solution.py:53
  117.6 3.9 %add_convert_fusion = bf16[1024,1024]{1,0:T(8,128)(2,1)S(1)} fusion(bf16[1024,1024]{1,0:T(8,128)(2,1)} %collective-permute-done, bf16[1024,768]{1,0:T(8,128)(2,1)S(1)} %bitcast.30, bf16[2048,768]{1,0:T(8,128)(2,1)} %all-gather.4.cloned.1.call-done, s32[]{:T(128)S(6)} %select_n.18), kind=kOutput, calls=%fused_computation.3 | convolution fusion | flops 1613758464 | bytes 7340036 | tf_op jit(solution)/shard_map/dot_general | solution.py:54
  121.5 29.2 %all_to_all.33 = bf16[4,256,1024]{2,1,0:T(8,128)(2,1)S(1)} all-to-all(bf16[4,256,1024]{2,1,0:T(8,128)(2,1)S(1)} %bitcast.26), channel_id=1, replica_groups=mesh['y'=4,'z'=8,'x'=4,'k'=2] {'x'}, dimensions={0} | all-to-all | bytes 4194304 | tf_op jit(solution)/shard_map/all_to_all | solution.py:56
  151.2 0.8 collective-permute-start.1
  152.0 0.7 dynamic_slice.21
  152.7 3.2 %multiply_reduce_fusion = f32[256]{0:T(256)S(1)} fusion(bf16[256,8192]{1,0:T(8,128)(2,1)} %param.7), kind=kLoop, calls=%fused_computation | loop fusion | flops 6291200 | bytes 4195328 | tf_op jit(solution)/shard_map/reduce_sum | solution.py:62
  155.9 1.3 fusion.12
  157.2 0.6 broadcast_in_dim.13
  157.8 28.6 %all-to-all-start.2 = ((f32[8,1,256]{2,1,0:T(1,128)}), f32[8,1,256]{2,1,0:T(1,128)S(1)}, u32[]{:S(2)}, u32[]{:S(2)}) async-start(f32[8,1,256]{2,1,0:T(1,128)} %broadcast_in_dim.13), calls=%async_computation.2 | async-start | bytes 16384 | tf_op jit(solution)/shard_map/all_to_all | solution.py:20
  186.5 1.9 fusion.17
  188.4 0.8 dynamic-slice_divide_fusion
  189.2 0.7 pad_bitcast_fusion
  189.8 1.2 all-to-all-done.2
  191.7 3.9 %all-to-all-start.4 = ((f32[8,3,128]{2,1,0:T(4,128)}), f32[8,3,128]{2,1,0:T(4,128)S(1)}, u32[]{:S(2)}, u32[]{:S(2)}) async-start(f32[8,3,128]{2,1,0:T(4,128)} %broadcast_in_dim.16), calls=%async_computation.5 | async-start | bytes 32768 | tf_op jit(solution)/shard_map/all_to_all | solution.py:20
  195.7 4.6 %all-to-all-done.4 = f32[8,3,128]{2,1,0:T(4,128)S(1)} async-done(((f32[8,3,128]{2,1,0:T(4,128)}), f32[8,3,128]{2,1,0:T(4,128)S(1)}, u32[]{:S(2)}, u32[]{:S(2)}) %all-to-all-start.4) | async-done | bytes 12320 | tf_op jit(solution)/shard_map/all_to_all | solution.py:20
  200.3 0.6 broadcast_in_dim.17
  200.9 7.4 %all-to-all-start.5 = ((f32[32,3,128]{2,1,0:T(4,128)}), f32[32,3,128]{2,1,0:T(4,128)S(1)}, u32[]{:S(2)}, u32[]{:S(2)}) async-start(f32[32,3,128]{2,1,0:T(4,128)} %broadcast_in_dim.17), calls=%async_computation.6 | async-start | bytes 131072 | tf_op jit(solution)/shard_map/all_to_all | solution.py:20
  208.4 2.3 fusion.11
  210.7 0.7 slice.16
  211.4 0.7 slice.17
  212.1 5.2 %all-to-all-done.5 = f32[32,3,128]{2,1,0:T(4,128)S(1)} async-done(((f32[32,3,128]{2,1,0:T(4,128)}), f32[32,3,128]{2,1,0:T(4,128)S(1)}, u32[]{:S(2)}, u32[]{:S(2)}) %all-to-all-start.5) | async-done | bytes 49184 | tf_op jit(solution)/shard_map/all_to_all | solution.py:20
  217.9 0.7 slice_reduce_fusion
  (39 shorter events, 3.4 us)
Async XLA Ops:
  7.2 16.3 %copy-start.5 = (bf16[256,512]{1,0:T(8,128)(2,1)S(1)}, bf16[256,512]{1,0:T(8,128)(2,1)}, u32[]{:S(2)}) copy-start(bf16[256,512]{1,0:T(8,128)(2,1)} %param.11) | copy-start | bytes 786436
  7.2 16.3 %copy-start.6 = (bf16[256,256]{1,0:T(8,128)(2,1)S(1)}, bf16[256,256]{1,0:T(8,128)(2,1)}, u32[]{:S(2)}) copy-start(bf16[256,256]{1,0:T(8,128)(2,1)} %param.12) | copy-start | bytes 393220
  7.2 54.1 %all-gather.6.cloned.1.call-start = ((), (), s32[]{:S(2)}) async-start(), calls=%async_computation.9 | async-start | bytes 4718592 | tf_op jit(solution)/shard_map/all_gather | solution.py:46
  7.2 17.1 %copy-start.4 = (bf16[256,512]{1,0:T(8,128)(2,1)S(1)}, bf16[256,512]{1,0:T(8,128)(2,1)}, u32[]{:S(2)}) copy-start(bf16[256,512]{1,0:T(8,128)(2,1)} %param.9) | copy-start | bytes 786436
  7.3 17.1 %copy-start.7 = (bf16[256,256]{1,0:T(8,128)(2,1)S(1)}, bf16[256,256]{1,0:T(8,128)(2,1)}, u32[]{:S(2)}) copy-start(bf16[256,256]{1,0:T(8,128)(2,1)} %param.10) | copy-start | bytes 393220
  23.4 84.3 %all-gather.4.cloned.1.call-start = ((), (), s32[]{:S(2)}) async-start(), calls=%async_computation.7 | async-start | bytes 3538944 | tf_op jit(solution)/shard_map/all_gather | solution.py:35
  23.5 0.7 copy-start
  24.3 162.2 %reduce-scatter.2.cloned.1.call-start = ((), (), s32[]{:S(2)}) async-start(), calls=%async_computation.8 | async-start | bytes 3538944 | tf_op jit(solution)/shard_map/reduce_scatter | solution.py:83
  112.2 5.4 %collective-permute-start = (bf16[1024,1024]{1,0:T(8,128)(2,1)}, bf16[1024,1024]{1,0:T(8,128)(2,1)}, u32[]{:S(2)}, u32[]{:S(2)}) collective-permute-start(bf16[1024,1024]{1,0:T(8,128)(2,1)} %convolution_convert_fusion), channel_id=1, source_target_pairs={{0,1},{1,0},{2,3},{3,2},{4,5},{5,4},{6,7},{7,6},{8,9},{9,8},{10,11... | collective-permute-start | bytes 6291464 | tf_op jit(solution)/shard_map/ppermute | solution.py:53
  151.2 35.3 %copy-start.1 = (bf16[256,768]{1,0:T(8,128)(2,1)S(1)}, bf16[256,768]{1,0:T(8,128)(2,1)}, u32[]{:S(2)}) copy-start(bf16[256,768]{1,0:T(8,128)(2,1)} %copy-done) | copy-start | bytes 1179652
  151.2 4.7 %collective-permute-start.1 = (bf16[256,1024]{1,0:T(8,128)(2,1)S(1)}, bf16[256,1024]{1,0:T(8,128)(2,1)S(1)}, u32[]{:S(2)}, u32[]{:S(2)}) collective-permute-start(bf16[256,1024]{1,0:T(8,128)(2,1)S(1)} %reduce_sum.94), channel_id=1, source_target_pairs={{0,0},{2,64},{4,128},{6,192},{64,2},{66,66},{68,130},{70,194},{128... | collective-permute-start | bytes 1572872 | tf_op jit(solution)/shard_map/ppermute | solution.py:59
  152.7 55.7 %copy-start.3 = (bf16[256,1024]{1,0:T(8,128)(2,1)S(1)}, bf16[256,1024]{1,0:T(8,128)(2,1)}, u32[]{:S(2)}) copy-start(bf16[256,1024]{1,0:T(8,128)(2,1)} %param.13) | copy-start | bytes 1572868
  157.8 33.2 %all-to-all-start.2 = ((f32[8,1,256]{2,1,0:T(1,128)}), f32[8,1,256]{2,1,0:T(1,128)S(1)}, u32[]{:S(2)}, u32[]{:S(2)}) async-start(f32[8,1,256]{2,1,0:T(1,128)} %broadcast_in_dim.13), calls=%async_computation.2 | async-start | bytes 16384 | tf_op jit(solution)/shard_map/all_to_all | solution.py:20
  186.5 24.2 %copy-start.2 = (bf16[256,768]{1,0:T(8,128)(2,1)S(1)}, bf16[256,768]{1,0:T(8,128)(2,1)}, u32[]{:S(2)}) copy-start(bf16[256,768]{1,0:T(8,128)(2,1)} %reduce-scatter.2.cloned.1.call-done) | copy-start | bytes 1179652
  191.7 8.6 %all-to-all-start.4 = ((f32[8,3,128]{2,1,0:T(4,128)}), f32[8,3,128]{2,1,0:T(4,128)S(1)}, u32[]{:S(2)}, u32[]{:S(2)}) async-start(f32[8,3,128]{2,1,0:T(4,128)} %broadcast_in_dim.16), calls=%async_computation.5 | async-start | bytes 32768 | tf_op jit(solution)/shard_map/all_to_all | solution.py:20
  200.9 16.3 %all-to-all-start.5 = ((f32[32,3,128]{2,1,0:T(4,128)}), f32[32,3,128]{2,1,0:T(4,128)S(1)}, u32[]{:S(2)}, u32[]{:S(2)}) async-start(f32[32,3,128]{2,1,0:T(4,128)} %broadcast_in_dim.17), calls=%async_computation.6 | async-start | bytes 131072 | tf_op jit(solution)/shard_map/all_to_all | solution.py:20
Sparse Core Ops, SparseCore 0:
  23.5 37.7 all-gather.5
  63.7 44.0 all-gather.3
  110.3 43.1 reduce-scatter.1
